TPU v7x, 32 devices: a whole 2x2x4 slice. The times are simulated.
32 devices in a mesh: col: 16 (over z, x, core), row: 2 (over y).
Axes of the slice: x: 2, y: 2, z: 4, core: 2. Of those that a mesh axis runs over, the one named last changes fastest.
Arguments:
- blocks: float32 [16, 2, 24, 128, 128], P('col', 'row'), may hold values from -0.21875 to 0.21875
- row_index: int32 [16, 2, 24], P('col', 'row'), may hold values from 0 to 63
- col_index: int32 [16, 2, 24], P('col', 'row'), may hold values from 0 to 23
- counts: int32 [16, 2], P('col', 'row'), may hold values from 12 to 24, as said below
- rhs: float32 [16384], P(('row', 'col')), may hold values from -6 to 6
- lower: float32 [49152], P(('col', 'row')), may hold values from -0.6 to -0.05
- upper: float32 [49152], P(('col', 'row')), may hold values from 0.05 to 0.6
- primal_start: float32 [49152], P(('col', 'row')), may hold values from -0.05 to 0.05
- dual_start: float32 [16384], P(('row', 'col')), may hold values from -4 to 4
Outputs:
- primal: float32 [49152], P(('col', 'row'))
- dual: float32 [16384], P(('row', 'col'))
- norms: float32 [3, 2], replicated
Inputs may be any that keep to these rules, and one draw needn't show every extreme that they name: `counts`: each list has between 12 and 24 live slots; both ends are reached in every draw.
All inputs are finite; a program needn't handle non-finite values.
Results may differ from a plain program's by a relative error of at most 0.0001.
Values sent between devices are 32-bit elements; how exact they have to be, the bound alone decides.
A program may use at most 64 MiB of HBM per device.

v0:
```python
import jax
import jax.numpy as jnp
from jax import lax
from jax.sharding import PartitionSpec as P

ITERS = 3


def local(blocks, row_index, col_index, counts, rhs, lower, upper, primal_start, dual_start):
    slot_count = blocks.shape[2]
    side = blocks.shape[3]
    tiles = blocks.reshape(slot_count, side, side)
    rows = row_index.reshape(slot_count)
    cols = col_index.reshape(slot_count)
    live = (jnp.arange(slot_count, dtype=jnp.int32) < counts.reshape(())).astype(jnp.float32)
    n_col = lax.axis_size("col")
    n_row = lax.axis_size("row")
    primal_len = primal_start.shape[0]
    dual_len = dual_start.shape[0]
    col_blocks = primal_len * n_row // side
    row_blocks = dual_len * n_col // side
    tau = 0.4
    sigma = 0.4
    records = []

    def record(resid_sq, moved_sq):
        total_resid, total_moved = lax.psum((resid_sq, moved_sq), ("col", "row"))
        records.append(jnp.stack([jnp.sqrt(total_resid), jnp.sqrt(total_moved)]))

    primal_group, lower_group, upper_group = (
        lax.all_gather(primal_start, "row", axis=0, tiled=True),
        lax.all_gather(lower, "row", axis=0, tiled=True),
        lax.all_gather(upper, "row", axis=0, tiled=True),
    )
    dual_group, rhs_group = (
        lax.all_gather(dual_start, "col", axis=0, tiled=True),
        lax.all_gather(rhs, "col", axis=0, tiled=True),
    )
    primal_offset = lax.axis_index("row") * primal_len
    dual_offset = lax.axis_index("col") * dual_len
    for step in range(ITERS):
        pieces = dual_group.reshape(-1, side)[rows]
        prod = (
            jnp.einsum("kij,ki->kj", tiles, pieces, precision=lax.Precision.HIGHEST) * live[:, None]
        )
        grad = lax.psum(jax.ops.segment_sum(prod, cols, num_segments=col_blocks).reshape(-1), "row")
        primal_new = jnp.minimum(jnp.maximum(primal_group + tau * grad, lower_group), upper_group)
        extra = 2.0 * primal_new - primal_group
        apply_pieces = extra.reshape(-1, side)[cols]
        apply_prod = (
            jnp.einsum("kij,kj->ki", tiles, apply_pieces, precision=lax.Precision.HIGHEST)
            * live[:, None]
        )
        product = lax.psum(
            jax.ops.segment_sum(apply_prod, rows, num_segments=row_blocks).reshape(-1), "col"
        )
        resid = rhs_group - product
        dual_group = dual_group + sigma * resid
        moved_own = lax.dynamic_slice_in_dim(primal_new - primal_group, primal_offset, primal_len)
        resid_own = lax.dynamic_slice_in_dim(resid, dual_offset, dual_len)
        record(jnp.sum(resid_own * resid_own), jnp.sum(moved_own * moved_own))
        primal_group = primal_new
    primal_out = lax.dynamic_slice_in_dim(primal_group, primal_offset, primal_len)
    dual_out = lax.dynamic_slice_in_dim(dual_group, dual_offset, dual_len)
    norms = jnp.stack(records)
    return (primal_out, dual_out, norms)


def solution(mesh):
    in_specs = (
        P("col", "row", None, None, None),
        P("col", "row", None),
        P("col", "row", None),
        P("col", "row"),
        P(("row", "col")),
        P(("col", "row")),
        P(("col", "row")),
        P(("col", "row")),
        P(("row", "col")),
    )
    out_specs = (P(("col", "row")), P(("row", "col")), P())
    return jax.shard_map(local, mesh=mesh, in_specs=in_specs, out_specs=out_specs, check_vma=False)
```

profile of v0, /device:TPU:12, one launch (start us, length us, event | category | flops | bytes accessed | tf_op | source)
XLA Modules:
  0.0 322.5 jit_solution(8826910674664493860)
XLA Ops:
  0.7 0.8 reshape.230
  1.5 4.4 %all-gather = f32[2,1,1536]{2,1,0:T(1,128)S(1)} all-gather(f32[1,1,1536]{2,1,0:T(1,128)S(1)} %reshape.230), channel_id=1, replica_groups=mesh['col'=16,'row'=2] {'row'}, dimensions={0}, use_global_device_ids=true | all-gather | bytes 18432 | tf_op jit(solution)/shard_map/all_gather | solution.py:31
  5.9 0.7 reshape.236
  6.6 4.4 %all-gather.3 = f32[2,1,1536]{2,1,0:T(1,128)S(1)} all-gather(f32[1,1,1536]{2,1,0:T(1,128)S(1)} %reshape.236), channel_id=1, replica_groups=mesh['col'=16,'row'=2] {'row'}, dimensions={0}, use_global_device_ids=true | all-gather | bytes 18432 | tf_op jit(solution)/shard_map/all_gather | solution.py:33
  10.9 0.7 reshape.234
  11.6 4.4 %all-gather.2 = f32[2,1,1536]{2,1,0:T(1,128)S(1)} all-gather(f32[1,1,1536]{2,1,0:T(1,128)S(1)} %reshape.234), channel_id=1, replica_groups=mesh['col'=16,'row'=2] {'row'}, dimensions={0}, use_global_device_ids=true | all-gather | bytes 18432 | tf_op jit(solution)/shard_map/all_gather | solution.py:32
  16.0 19.1 %all-gather.1 = f32[16,1,512]{2,1,0:T(1,128)S(1)} all-gather(f32[1,1,512]{2,1,0:T(1,128)} %bitcast.129), channel_id=1, replica_groups=mesh['col'=16,'row'=2] {'col'}, dimensions={0}, use_global_device_ids=true | all-gather | bytes 34816 | tf_op jit(solution)/shard_map/all_gather | solution.py:36
  35.1 0.7 fusion.39
  36.4 1.4 fusion.10
  38.4 0.7 scatter_custom_fusion
  39.2 7.1 %psum.84 = f32[3072]{0:T(1024)S(1)} all-reduce(f32[3072]{0:T(1024)S(1)} %bitcast.126), channel_id=1, replica_groups=mesh['col'=16,'row'=2] {'row'}, use_global_device_ids=true, to_apply=%region_1.0 | all-reduce | flops 3072 | bytes 24576 | tf_op jit(solution)/shard_map/psum | solution.py:46
  46.3 17.2 %all-gather.4 = f32[16,1,512]{2,1,0:T(1,128)S(1)} all-gather(f32[1,1,512]{2,1,0:T(1,128)S(1)} %bitcast.130), channel_id=1, replica_groups=mesh['col'=16,'row'=2] {'col'}, dimensions={0}, use_global_device_ids=true | all-gather | bytes 34816 | tf_op jit(solution)/shard_map/all_gather | solution.py:37
  64.1 2.5 fusion.8
  66.6 0.9 scatter_custom_fusion.1
  67.5 54.3 %psum.85 = f32[8192]{0:T(1024)S(1)} all-reduce(f32[8192]{0:T(1024)S(1)} %bitcast.110), channel_id=1, replica_groups=mesh['col'=16,'row'=2] {'col'}, use_global_device_ids=true, to_apply=%region_3.0 | all-reduce | flops 8192 | bytes 65536 | tf_op jit(solution)/shard_map/psum | solution.py:54
  122.4 1.4 fusion.6
  123.8 0.7 scatter_custom_fusion.2
  124.5 8.1 %psum.86 = f32[3072]{0:T(1024)S(1)} all-reduce(f32[3072]{0:T(1024)S(1)} %bitcast.127), channel_id=1, replica_groups=mesh['col'=16,'row'=2] {'row'}, use_global_device_ids=true, to_apply=%region_5.0 | all-reduce | flops 3072 | bytes 24576 | tf_op jit(solution)/shard_map/psum | solution.py:46
  133.2 2.5 fusion.4
  135.8 0.9 scatter_custom_fusion.3
  136.7 57.6 %psum.87 = f32[8192]{0:T(1024)S(1)} all-reduce(f32[8192]{0:T(1024)S(1)} %bitcast.111), channel_id=1, replica_groups=mesh['col'=16,'row'=2] {'col'}, use_global_device_ids=true, to_apply=%region_7.0 | all-reduce | flops 8192 | bytes 65536 | tf_op jit(solution)/shard_map/psum | solution.py:54
  194.9 1.4 fusion.2
  196.3 0.7 scatter_custom_fusion.4
  197.0 7.1 %psum.88 = f32[3072]{0:T(1024)S(1)} all-reduce(f32[3072]{0:T(1024)S(1)} %bitcast.128), channel_id=1, replica_groups=mesh['col'=16,'row'=2] {'row'}, use_global_device_ids=true, to_apply=%region_9.0 | all-reduce | flops 3072 | bytes 24576 | tf_op jit(solution)/shard_map/psum | solution.py:46
  204.1 1.3 fusion.29
  206.1 2.5 fusion
  208.6 0.9 scatter_custom_fusion.5
  209.5 57.6 %psum.89 = f32[8192]{0:T(1024)S(1)} all-reduce(f32[8192]{0:T(1024)S(1)} %bitcast.109), channel_id=1, replica_groups=mesh['col'=16,'row'=2] {'col'}, use_global_device_ids=true, to_apply=%region_11.0 | all-reduce | flops 8192 | bytes 65536 | tf_op jit(solution)/shard_map/psum | solution.py:54
  267.1 1.3 multiply_reduce_fusion.2
  268.4 0.7 multiply_reduce_fusion.4
  269.1 48.5 %all-reduce = (f32[]{:T(128)}, f32[]{:T(128)}, f32[]{:T(128)}, f32[]{:T(128)}, f32[]{:T(128)}, /*index=5*/f32[]{:T(128)}) all-reduce(f32[]{:T(128)} %get-tuple-element.11, f32[]{:T(128)} %get-tuple-element.29, f32[]{:T(128)} %get-tuple-element.10, f32[]{:T(128)} %get-tuple-element.31, ...), channel_id=1, replica_groups=mesh['col'=16,'row'=2] {'col','row'}, use_global_device_ids=true, to_apply=%region_23.0 | all-reduce | flops 6 | bytes 48 | tf_op jit(solution)/shard_map/psum | solution.py:27
  321.9 0.7 copy.13
  (26 shorter events, 3.7 us)
Async XLA Ops:
  0.6 35.7 %copy-start = (f32[1,1,24,128,128]{4,3,2,1,0:T(8,128)S(1)}, f32[1,1,24,128,128]{4,3,2,1,0:T(8,128)}, u32[]{:S(2)}) copy-start(f32[1,1,24,128,128]{4,3,2,1,0:T(8,128)} %param.9) | copy-start | bytes 4718596
  0.6 37.8 %copy-start.2 = (s32[1,1,24]{2,1,0:T(1,128)S(1)}, s32[1,1,24]{2,1,0:T(1,128)}, u32[]{:S(2)}) copy-start(s32[1,1,24]{2,1,0:T(1,128)} %param.11) | copy-start | bytes 292
  0.7 45.6 %copy-start.1 = (f32[512]{0:T(512)S(1)}, f32[512]{0:T(512)}, u32[]{:S(2)}) copy-start(f32[512]{0:T(512)} %param.13) | copy-start | bytes 6148
where the time goes:
time: 323 us
  blocking collectives  290 us (90%)
  matrix products  11.9 us (4%)
  other arithmetic  9.14 us (3%)
  local copies, waits for them, and re-layouts  6.29 us (2%)
  between operations  5.46 us (2%)
    psum x3, blocking collectives, local(): lax.psum(jax.ops.segment_sum(apply_prod, rows, num_segments=row_blocks).r...  170 us
    psum x1, blocking collectives, record(): total_resid, total_moved = lax.psum((resid_sq, moved_sq), ('col', 'row'))  48.5 us
    psum x3, blocking collectives, local(): lax.psum(jax.ops.segment_sum(prod, cols, num_segments=col_blocks).reshape...  22.3 us
    all_gather x1, blocking collectives, local(): lax.all_gather(dual_start, 'col', axis=0, tiled=True)  19.1 us
    all_gather x1, blocking collectives, local(): lax.all_gather(rhs, 'col', axis=0, tiled=True)  17.2 us
    dot_general x3, matrix products, local(): jnp.einsum('kij,kj->ki', tiles, apply_pieces, precision=lax.Precision.HIG...  7.62 us

commit v1 on v0

--- a/solution.py
+++ b/solution.py
@@ -43,7 +43,9 @@
         prod = (
             jnp.einsum("kij,ki->kj", tiles, pieces, precision=lax.Precision.HIGHEST) * live[:, None]
         )
-        grad = lax.psum(jax.ops.segment_sum(prod, cols, num_segments=col_blocks).reshape(-1), "row")
+        grad = jax.lax.all_gather(
+            jax.ops.segment_sum(prod, cols, num_segments=col_blocks).reshape(-1), "row"
+        ).sum(axis=0)
         primal_new = jnp.minimum(jnp.maximum(primal_group + tau * grad, lower_group), upper_group)
         extra = 2.0 * primal_new - primal_group
         apply_pieces = extra.reshape(-1, side)[cols]

time: 323 us -> 313 us (0.969)
  blocking collectives: 290 us -> 280 us
    psum x3 -> x0, blocking collectives: 22.3 us -> none  [local(): lax.psum(jax.ops.segment_sum(prod, cols, num_segments=col_blocks).reshape...]
    all_gather x0 -> x3, blocking collectives: none -> 13.2 us  [local(): jax.lax.all_gather(jax.ops.segment_sum(prod, cols, num_segments=col_block...]
where the time goes in v1:
time: 313 us
  blocking collectives  280 us (89%)
  matrix products  11.9 us (4%)
  other arithmetic  9.25 us (3%)
  local copies, waits for them, and re-layouts  6.29 us (2%)
  between operations  5.49 us (2%)
    psum x3, blocking collectives, local(): lax.psum(jax.ops.segment_sum(apply_prod, rows, num_segments=row_blocks).r...  170 us
    psum x1, blocking collectives, record(): total_resid, total_moved = lax.psum((resid_sq, moved_sq), ('col', 'row'))  47.5 us
    all_gather x1, blocking collectives, local(): lax.all_gather(dual_start, 'col', axis=0, tiled=True)  19.1 us
    all_gather x1, blocking collectives, local(): lax.all_gather(rhs, 'col', axis=0, tiled=True)  17.2 us
    all_gather x3, blocking collectives, local(): jax.lax.all_gather(jax.ops.segment_sum(prod, cols, num_segments=col_block...  13.2 us
    dot_general x3, matrix products, local(): jnp.einsum('kij,kj->ki', tiles, apply_pieces, precision=lax.Precision.HIG...  7.62 us

profile of v1, /device:TPU:12, one launch (start us, length us, event | category | flops | bytes accessed | tf_op | source)
XLA Modules:
  0.0 312.6 jit_solution(9000711618814326744)
XLA Ops:
  0.7 0.8 reshape.218
  1.5 4.4 %all-gather = f32[2,1,1536]{2,1,0:T(1,128)S(1)} all-gather(f32[1,1,1536]{2,1,0:T(1,128)S(1)} %reshape.218), channel_id=1, replica_groups=mesh['col'=16,'row'=2] {'row'}, dimensions={0}, use_global_device_ids=true | all-gather | bytes 18432 | tf_op jit(solution)/shard_map/all_gather | solution.py:31
  5.9 0.7 reshape.226
  6.6 4.4 %all-gather.4 = f32[2,1,1536]{2,1,0:T(1,128)S(1)} all-gather(f32[1,1,1536]{2,1,0:T(1,128)S(1)} %reshape.226), channel_id=1, replica_groups=mesh['col'=16,'row'=2] {'row'}, dimensions={0}, use_global_device_ids=true | all-gather | bytes 18432 | tf_op jit(solution)/shard_map/all_gather | solution.py:33
  10.9 0.7 reshape.224
  11.6 4.4 %all-gather.3 = f32[2,1,1536]{2,1,0:T(1,128)S(1)} all-gather(f32[1,1,1536]{2,1,0:T(1,128)S(1)} %reshape.224), channel_id=1, replica_groups=mesh['col'=16,'row'=2] {'row'}, dimensions={0}, use_global_device_ids=true | all-gather | bytes 18432 | tf_op jit(solution)/shard_map/all_gather | solution.py:32
  16.0 19.1 %all-gather.1 = f32[16,1,512]{2,1,0:T(1,128)S(1)} all-gather(f32[1,1,512]{2,1,0:T(1,128)} %bitcast.129), channel_id=1, replica_groups=mesh['col'=16,'row'=2] {'col'}, dimensions={0}, use_global_device_ids=true | all-gather | bytes 34816 | tf_op jit(solution)/shard_map/all_gather | solution.py:36
  35.1 0.7 fusion.39
  36.4 1.4 fusion.10
  38.4 0.7 scatter_custom_fusion
  39.2 4.4 %all-gather.2 = f32[2,1,3072]{2,1,0:T(1,128)S(1)} all-gather(f32[1,1,3072]{2,1,0:T(1,128)S(1)} %bitcast.126), channel_id=1, replica_groups=mesh['col'=16,'row'=2] {'row'}, dimensions={0}, use_global_device_ids=true | all-gather | bytes 36864 | tf_op jit(solution)/shard_map/all_gather | solution.py:46
  43.6 17.2 %all-gather.5 = f32[16,1,512]{2,1,0:T(1,128)S(1)} all-gather(f32[1,1,512]{2,1,0:T(1,128)S(1)} %bitcast.130), channel_id=1, replica_groups=mesh['col'=16,'row'=2] {'col'}, dimensions={0}, use_global_device_ids=true | all-gather | bytes 34816 | tf_op jit(solution)/shard_map/all_gather | solution.py:37
  61.4 2.5 fusion.8
  64.0 0.9 scatter_custom_fusion.1
  64.9 54.3 %psum.63 = f32[8192]{0:T(1024)S(1)} all-reduce(f32[8192]{0:T(1024)S(1)} %bitcast.110), channel_id=1, replica_groups=mesh['col'=16,'row'=2] {'col'}, use_global_device_ids=true, to_apply=%region_3.0 | all-reduce | flops 8192 | bytes 65536 | tf_op jit(solution)/shard_map/psum | solution.py:56
  119.7 1.4 fusion.6
  121.1 0.7 scatter_custom_fusion.2
  121.9 4.4 %all-gather.6 = f32[2,1,3072]{2,1,0:T(1,128)S(1)} all-gather(f32[1,1,3072]{2,1,0:T(1,128)S(1)} %bitcast.127), channel_id=1, replica_groups=mesh['col'=16,'row'=2] {'row'}, dimensions={0}, use_global_device_ids=true | all-gather | bytes 36864 | tf_op jit(solution)/shard_map/all_gather | solution.py:46
  126.9 2.5 fusion.4
  129.4 0.9 scatter_custom_fusion.3
  130.3 57.6 %psum.64 = f32[8192]{0:T(1024)S(1)} all-reduce(f32[8192]{0:T(1024)S(1)} %bitcast.111), channel_id=1, replica_groups=mesh['col'=16,'row'=2] {'col'}, use_global_device_ids=true, to_apply=%region_7.0 | all-reduce | flops 8192 | bytes 65536 | tf_op jit(solution)/shard_map/psum | solution.py:56
  188.6 1.4 fusion.2
  190.0 0.7 scatter_custom_fusion.4
  190.7 4.4 %all-gather.7 = f32[2,1,3072]{2,1,0:T(1,128)S(1)} all-gather(f32[1,1,3072]{2,1,0:T(1,128)S(1)} %bitcast.128), channel_id=1, replica_groups=mesh['col'=16,'row'=2] {'row'}, dimensions={0}, use_global_device_ids=true | all-gather | bytes 36864 | tf_op jit(solution)/shard_map/all_gather | solution.py:46
  195.2 1.4 fusion.29
  197.1 2.5 fusion
  199.6 0.9 scatter_custom_fusion.5
  200.5 57.6 %psum.65 = f32[8192]{0:T(1024)S(1)} all-reduce(f32[8192]{0:T(1024)S(1)} %bitcast.109), channel_id=1, replica_groups=mesh['col'=16,'row'=2] {'col'}, use_global_device_ids=true, to_apply=%region_11.0 | all-reduce | flops 8192 | bytes 65536 | tf_op jit(solution)/shard_map/psum | solution.py:56
  258.2 1.3 multiply_reduce_fusion.2
  259.4 0.7 multiply_reduce_fusion.4
  260.1 47.5 %all-reduce = (f32[]{:T(128)}, f32[]{:T(128)}, f32[]{:T(128)}, f32[]{:T(128)}, f32[]{:T(128)}, /*index=5*/f32[]{:T(128)}) all-reduce(f32[]{:T(128)} %get-tuple-element.11, f32[]{:T(128)} %get-tuple-element.29, f32[]{:T(128)} %get-tuple-element.10, f32[]{:T(128)} %get-tuple-element.31, ...), channel_id=1, replica_groups=mesh['col'=16,'row'=2] {'col','row'}, use_global_device_ids=true, to_apply=%region_23.0 | all-reduce | flops 6 | bytes 48 | tf_op jit(solution)/shard_map/psum | solution.py:27
  311.9 0.7 copy.13
  (29 shorter events, 3.9 us)
Async XLA Ops:
  0.6 35.7 %copy-start = (f32[1,1,24,128,128]{4,3,2,1,0:T(8,128)S(1)}, f32[1,1,24,128,128]{4,3,2,1,0:T(8,128)}, u32[]{:S(2)}) copy-start(f32[1,1,24,128,128]{4,3,2,1,0:T(8,128)} %param.9) | copy-start | bytes 4718596
  0.6 37.8 %copy-start.2 = (s32[1,1,24]{2,1,0:T(1,128)S(1)}, s32[1,1,24]{2,1,0:T(1,128)}, u32[]{:S(2)}) copy-start(s32[1,1,24]{2,1,0:T(1,128)} %param.11) | copy-start | bytes 292
  0.7 43.0 %copy-start.1 = (f32[512]{0:T(512)S(1)}, f32[512]{0:T(512)}, u32[]{:S(2)}) copy-start(f32[512]{0:T(512)} %param.13) | copy-start | bytes 6148
